TPU v7x, 32 devices: a whole 2x2x4 slice. The times are simulated.
32 devices in a mesh: tab: 8 (over z, x), rep: 4 (over y, core).
Axes of the slice: x: 2, y: 2, z: 4, core: 2. Of those that a mesh axis runs over, the one named last changes fastest.
Arguments:
- sample_ids: int32 [16384, 26], P(('tab', 'rep')), may hold values from 0 to 4095, as said below
- features: bfloat16 [16384, 27, 128], P(('tab', 'rep')), may hold values from -6 to 6
- pair_grad: bfloat16 [351, 16384], P(None, ('tab', 'rep')), may hold values from -1.59375 to 1.59375
Outputs:
- table_grad: float32 [26, 4096, 128], P(None, ('tab', 'rep'))
- dense_grad: float32 [16384, 128], P(('tab', 'rep'))
Inputs may be any that keep to these rules, and one draw needn't show every extreme that they name: `sample_ids`: row r is owned by device r // 128, numbered tab * 4 + rep. For each field and the 512 samples of one device (aligned blocks of rows in device order), at most 32 ids fall in the rows of any one device, and at most 128 in the rows of any one tab index; in every block and field both bounds are reached.
All inputs are finite; a program needn't handle non-finite values.
Results may differ from a plain program's by a relative error of at most 0.0029.
Values may be sent and summed in bfloat16 or wider, within the bound.
No kernel may reach another device: no remote copies, remote signals or barrier semaphores. Data moves between devices by JAX's collectives and lax.ppermute only.
A program may use at most 128 MiB of HBM per device.

v0:
```python
import jax
import jax.numpy as jnp
import numpy as np
from jax import lax
from jax.sharding import PartitionSpec as P

RQ = 128


def pair_table(vectors):
    row_of, col_of = np.tril_indices(vectors, -1)
    spread = np.zeros((row_of.shape[0], vectors * vectors), np.float32)
    places = np.arange(row_of.shape[0])
    spread[places, row_of * vectors + col_of] = 1.0
    spread[places, col_of * vectors + row_of] = 1.0
    return spread


def arrival_order(targets, bins):
    matches = (targets[:, None] == jnp.arange(bins, dtype=jnp.int32)[None, :]).astype(jnp.int32)
    return jnp.sum(jnp.cumsum(matches, axis=0) * matches, axis=1) - 1


def place_field(slot_of, tag_of, grads, slot_total):
    placing = jnp.arange(slot_total, dtype=jnp.int32)[:, None] == slot_of[None, :]
    placed = jnp.dot(
        placing.astype(jnp.bfloat16), grads, preferred_element_type=jnp.float32
    ).astype(jnp.bfloat16)
    shifted = (tag_of + 1).astype(jnp.float32)
    tag_sum = jnp.dot(placing.astype(jnp.float32), shifted, precision=lax.Precision.HIGHEST)
    return (placed, tag_sum.astype(jnp.int32) - 1)


def tally_rows(arrived, row_tags, row_count):

    def per_field(pieces):
        slot_grads, slot_tags = pieces
        matches = (slot_tags[None, :] == jnp.arange(row_count, dtype=jnp.int32)[:, None]).astype(
            jnp.bfloat16
        )
        return jnp.dot(matches, slot_grads, preferred_element_type=jnp.float32)

    return lax.map(per_field, (arrived, row_tags))


def local(sample_ids, features, pair_grad):
    vectors = features.shape[1]
    samples = features.shape[0]
    depth = features.shape[2]
    spread = jnp.asarray(pair_table(vectors).T).astype(jnp.bfloat16)
    symmetric = jnp.dot(spread, pair_grad, preferred_element_type=jnp.float32)
    symmetric = symmetric.astype(jnp.bfloat16).reshape(vectors, vectors, samples)
    gradients = jnp.einsum("fgb,bge->fbe", symmetric, features, preferred_element_type=jnp.float32)
    dense_grad = gradients[0]
    field_grads = gradients[1:].astype(jnp.bfloat16)
    fields = vectors - 1
    col_count = lax.axis_size("tab")
    rep_count = lax.axis_size("rep")
    capacity = 2 * samples // (col_count * rep_count)
    slot_total = col_count * rep_count * capacity
    ids_by_field = sample_ids.T

    def build_owner(pieces):
        column_ids, grads = pieces
        owners = column_ids // RQ
        slot_of = owners * capacity + arrival_order(owners, col_count * rep_count)
        return place_field(slot_of, column_ids % RQ, grads, slot_total)

    outgoing, row_tags = lax.map(build_owner, (ids_by_field, field_grads))
    outgoing = outgoing.reshape(fields, col_count, rep_count, capacity, depth)
    row_tags = row_tags.reshape(fields, col_count, rep_count, capacity)
    arrived, tags_in = (
        lax.all_to_all(
            lax.all_to_all(outgoing, "tab", split_axis=1, concat_axis=1, tiled=True),
            "rep",
            split_axis=2,
            concat_axis=2,
            tiled=True,
        ),
        lax.all_to_all(
            lax.all_to_all(row_tags, "tab", split_axis=1, concat_axis=1, tiled=True),
            "rep",
            split_axis=2,
            concat_axis=2,
            tiled=True,
        ),
    )
    table_grad = tally_rows(arrived.reshape(fields, -1, depth), tags_in.reshape(fields, -1), RQ)
    return (table_grad, dense_grad)


def solution(mesh):
    placed = (P(("tab", "rep"), None), P(("tab", "rep"), None, None), P(None, ("tab", "rep")))
    return jax.shard_map(
        local,
        mesh=mesh,
        in_specs=placed,
        out_specs=(P(None, ("tab", "rep"), None), P(("tab", "rep"), None)),
        check_vma=False,
    )
```

profile of v0, /device:TPU:0, one launch (start us, length us, event | category | flops | bytes accessed | tf_op | source)
XLA Modules:
  0.0 536.2 jit_solution(541020844716352694)
XLA Ops:
  0.7 2.7 convolution_convert_fusion
  3.4 2.2 reshape.112
  5.6 7.5 %copy.20 = bf16[27,27,512]{1,0,2:T(8,128)(2,1)} copy(bf16[27,27,512]{2,1,0:T(8,128)(2,1)} %reshape.112) | data formatting | bytes 1492992 | tf_op jit(solution)/shard_map/reshape | solution.py:52
  13.1 4.5 fusion.25
  18.8 2.1 copy-done.2
  22.2 173.3 %while.25 = (s32[]{:T(128)}, bf16[26,1024,128]{2,1,0:T(8,128)(2,1)}, s32[26,1024]{1,0:T(8,128)}, s32[26,512]{1,0:T(8,128)}, bf16[26,512,128]{2,1,0:T(8,128)(2,1)S(1)}, /*index=5*/s32[]{:T(128)}, s32[]{:T(128)}) while((s32[]{:T(128)}, bf16[26,1024,128]{2,1,0:T(8,128)(2,1)}, s32[26,1024]{1,0:T(8,128)}, s32[26,512]{1,0:T(8,128)}, ...), condition=%wide.region_4.5_spmd, body=%wide.region_0.4_spmd.sunk | while | flops 143897568 | bytes 717545 | solution.py:69
  197.7 7.2 %all-to-all-start = ((s32[8,1,3328]{2,1,0:T(1,128)}), s32[8,1,3328]{2,1,0:T(1,128)S(1)}, u32[]{:S(2)}, u32[]{:S(2)}) async-start(s32[8,1,3328]{2,1,0:T(1,128)} %reshape.120), calls=%async_computation | async-start | bytes 212992 | tf_op jit(solution)/shard_map/all_to_all | solution.py:81
  205.0 8.6 %copy.26 = bf16[26,8,4,32,128]{4,3,2,0,1:T(8,128)(2,1)} copy(bf16[26,8,4,32,128]{4,3,2,1,0:T(8,128)(2,1)} %bitcast.88) | data formatting | bytes 13631488 | tf_op jit(solution)/shard_map/reshape | solution.py:70
  213.6 6.0 %all-to-all-start.2 = ((bf16[26,8,4,32,128]{4,3,2,0,1:T(8,128)(2,1)}), bf16[26,8,4,32,128]{4,3,2,0,1:T(8,128)(2,1)}, u32[]{:S(2)}, u32[]{:S(2)}) async-start(bf16[26,8,4,32,128]{4,3,2,0,1:T(8,128)(2,1)} %copy.26), calls=%async_computation.2 | async-start | bytes 13631488 | tf_op jit(solution)/shard_map/all_to_all | solution.py:74
  222.2 146.3 %all-to-all-done.2 = bf16[26,8,4,32,128]{4,3,2,0,1:T(8,128)(2,1)} async-done(((bf16[26,8,4,32,128]{4,3,2,0,1:T(8,128)(2,1)}), bf16[26,8,4,32,128]{4,3,2,0,1:T(8,128)(2,1)}, u32[]{:S(2)}, u32[]{:S(2)}) %all-to-all-start.2) | async-done | bytes 6815776 | tf_op jit(solution)/shard_map/all_to_all | solution.py:74
  368.5 3.5 all-to-all-start.1
  372.0 7.9 %copy.27 = bf16[26,8,4,32,128]{4,3,1,0,2:T(8,128)(2,1)} copy(bf16[26,8,4,32,128]{4,3,2,0,1:T(8,128)(2,1)} %all-to-all-done.2) | data formatting | bytes 13631488 | tf_op jit(solution)/shard_map/all_to_all | solution.py:74
  379.8 5.4 %all-to-all-start.3 = ((bf16[26,8,4,32,128]{4,3,1,0,2:T(8,128)(2,1)}), bf16[26,8,4,32,128]{4,3,1,0,2:T(8,128)(2,1)}, u32[]{:S(2)}, u32[]{:S(2)}) async-start(bf16[26,8,4,32,128]{4,3,1,0,2:T(8,128)(2,1)} %copy.27), calls=%async_computation.3 | async-start | bytes 13631488 | tf_op jit(solution)/shard_map/all_to_all | solution.py:73
  385.3 2.4 slice.25
  389.9 71.6 %all-to-all-done.3 = bf16[26,8,4,32,128]{4,3,1,0,2:T(8,128)(2,1)} async-done(((bf16[26,8,4,32,128]{4,3,1,0,2:T(8,128)(2,1)}), bf16[26,8,4,32,128]{4,3,1,0,2:T(8,128)(2,1)}, u32[]{:S(2)}, u32[]{:S(2)}) %all-to-all-start.3) | async-done | bytes 6815776 | tf_op jit(solution)/shard_map/all_to_all | solution.py:73
  461.6 8.0 %copy.28 = bf16[26,8,4,32,128]{4,3,2,1,0:T(8,128)(2,1)} copy(bf16[26,8,4,32,128]{4,3,1,0,2:T(8,128)(2,1)} %all-to-all-done.3) | data formatting | bytes 13631488 | tf_op jit(solution)/shard_map/all_to_all | solution.py:73
  469.6 66.7 %while.26 = (s32[]{:T(128)}, f32[26,128,128]{2,1,0:T(8,128)}, s32[26,1024]{1,0:T(8,128)}, bf16[26,1024,128]{2,1,0:T(8,128)(2,1)}, s32[]{:T(128)}) while((s32[]{:T(128)}, f32[26,128,128]{2,1,0:T(8,128)}, s32[26,1024]{1,0:T(8,128)}, bf16[26,1024,128]{2,1,0:T(8,128)(2,1)}, s32[]{:T(128)}) %tuple.59), condition=%wide.region_6.7_spmd, body=%wide.region_5.6_spmd.sunk | while | flops 33685504 | bytes 341065 | solution.py:43
  470.3 1.8 fusion.49
  472.9 1.8 fusion.49
  480.6 1.8 fusion.49
  483.1 1.8 fusion.49
  485.7 1.8 fusion.49
  490.8 1.8 fusion.49
  493.4 1.8 fusion.49
  501.1 1.8 fusion.49
  503.7 1.8 fusion.49
  506.2 1.8 fusion.49
  511.3 1.8 fusion.49
  521.6 1.8 fusion.49
  524.2 1.8 fusion.49
  526.7 1.8 fusion.49
  531.9 1.8 fusion.49
  (451 shorter events, 221.7 us)
Async XLA Ops:
  0.6 12.5 %copy-start = (bf16[512,27,128]{2,0,1:T(8,128)(2,1)S(1)}, bf16[512,27,128]{2,0,1:T(8,128)(2,1)}, u32[]{:S(2)}) copy-start(bf16[512,27,128]{2,0,1:T(8,128)(2,1)} %param.9) | copy-start | bytes 10616836
  17.7 3.2 copy-start.2
  197.7 15.9 %all-to-all-start = ((s32[8,1,3328]{2,1,0:T(1,128)}), s32[8,1,3328]{2,1,0:T(1,128)S(1)}, u32[]{:S(2)}, u32[]{:S(2)}) async-start(s32[8,1,3328]{2,1,0:T(1,128)} %reshape.120), calls=%async_computation | async-start | bytes 212992 | tf_op jit(solution)/shard_map/all_to_all | solution.py:81
  213.6 154.9 %all-to-all-start.2 = ((bf16[26,8,4,32,128]{4,3,2,0,1:T(8,128)(2,1)}), bf16[26,8,4,32,128]{4,3,2,0,1:T(8,128)(2,1)}, u32[]{:S(2)}, u32[]{:S(2)}) async-start(bf16[26,8,4,32,128]{4,3,2,0,1:T(8,128)(2,1)} %copy.26), calls=%async_computation.2 | async-start | bytes 13631488 | tf_op jit(solution)/shard_map/all_to_all | solution.py:74
  368.5 11.4 %all-to-all-start.1 = ((s32[4,1,6656]{2,1,0:T(1,128)}), s32[4,1,6656]{2,1,0:T(1,128)S(1)}, u32[]{:S(2)}, u32[]{:S(2)}) async-start(s32[4,1,6656]{2,1,0:T(1,128)} %reshape.122), calls=%async_computation.1 | async-start | bytes 212992 | tf_op jit(solution)/shard_map/all_to_all | solution.py:80
  379.8 81.7 %all-to-all-start.3 = ((bf16[26,8,4,32,128]{4,3,1,0,2:T(8,128)(2,1)}), bf16[26,8,4,32,128]{4,3,1,0,2:T(8,128)(2,1)}, u32[]{:S(2)}, u32[]{:S(2)}) async-start(bf16[26,8,4,32,128]{4,3,1,0,2:T(8,128)(2,1)} %copy.27), calls=%async_computation.3 | async-start | bytes 13631488 | tf_op jit(solution)/shard_map/all_to_all | solution.py:73
  461.5 74.7 %copy-start.1 = (bf16[512,27,128]{2,0,1:T(8,128)(2,1)S(1)}, bf16[512,27,128]{2,0,1:T(8,128)(2,1)}, u32[]{:S(2)}) copy-start(bf16[512,27,128]{2,0,1:T(8,128)(2,1)} %param.9) | copy-start | bytes 10616836
where the time goes:
time: 544 us; the launch traced here: 536 us
  waiting for transfers between devices  218 us (40%)
  local copies, waits for them, and re-layouts  128 us (24%)
  matrix products  111 us (20%)
  other arithmetic  56.4 us (10%)
  starting transfers between devices  22.1 us (4%)
    all_to_all x1, waiting for transfers between devices, local(): lax.all_to_all(outgoing, 'tab', split_axis=1, concat_axis=1, tiled=True)  146 us
    all_to_all x1, waiting for transfers between devices, local(): lax.all_to_all(lax.all_to_all(outgoing, 'tab', split_axis=1, concat_axis=...  71.6 us
    dot_general x26, matrix products, per_field(): return jnp.dot(matches, slot_grads, preferred_element_type=jnp.float32)  46.8 us
    dynamic_update_slice x26, local copies, waits for them, and re-layouts, local(): outgoing, row_tags = lax.map(build_owner, (ids_by_field, field_grads))  36.6 us
    another operation x52, other arithmetic  31.3 us
    dot_general x26, matrix products, place_field(): jnp.dot(placing.astype(jnp.bfloat16), grads, preferred_element_type=jnp.f...  30.5 us
    dot_general x26, matrix products, place_field(): jnp.dot(placing.astype(jnp.float32), shifted, precision=lax.Precision.HIG...  26.3 us
    dynamic_slice x26, local copies, waits for them, and re-layouts, tally_rows(): return lax.map(per_field, (arrived, row_tags))  19.9 us
  transfers between devices with their start and end apart: 4, of which 2 were waited for; matrix products, arithmetic and copies ran while one was open for 4% of the time, Pallas kernels for 0%

commit v1 on v0

--- a/solution.py
+++ b/solution.py
@@ -71,7 +71,12 @@
     row_tags = row_tags.reshape(fields, col_count, rep_count, capacity)
     arrived, tags_in = (
         lax.all_to_all(
-            lax.all_to_all(outgoing, "tab", split_axis=1, concat_axis=1, tiled=True),
+            jnp.concatenate(
+                lax.all_to_all(
+                    jnp.stack(jnp.split(outgoing, lax.axis_size("tab"), axis=1)), "tab", 0, 0
+                ),
+                axis=1,
+            ),
             "rep",
             split_axis=2,
             concat_axis=2,

time: 544 us -> 547 us (level)
    unnamed x10 -> x19, local copies, waits for them, and re-layouts: 4.29 us -> 14.8 us
    all_to_all x2 -> x1, local copies, waits for them, and re-layouts: 15.9 us -> 7.86 us  [local(): lax.all_to_all(jnp.concatenate(lax.all_to_all(jnp.stack(jnp.split(outgoin...]
  transfers between devices with their start and end apart: 4 -> 4, of which waited for: 2 -> 2; matrix products, arithmetic and copies ran while one was open for 4% -> 6% of each run, Pallas kernels for 0% -> 0%
where the time goes in v1:
time: 547 us; the launch traced here: 539 us
  waiting for transfers between devices  216 us (39%)
  local copies, waits for them, and re-layouts  132 us (24%)
  matrix products  111 us (20%)
  other arithmetic  56.4 us (10%)
  starting transfers between devices  22.1 us (4%)
    all_to_all x1, waiting for transfers between devices, local(): lax.all_to_all(jnp.stack(jnp.split(outgoing, lax.axis_size('tab'), axis=1...  146 us
    all_to_all x1, waiting for transfers between devices, local(): lax.all_to_all(jnp.concatenate(lax.all_to_all(jnp.stack(jnp.split(outgoin...  69.7 us
    dot_general x26, matrix products, per_field(): return jnp.dot(matches, slot_grads, preferred_element_type=jnp.float32)  46.8 us
    dynamic_update_slice x26, local copies, waits for them, and re-layouts, local(): outgoing, row_tags = lax.map(build_owner, (ids_by_field, field_grads))  36.6 us
    another operation x52, other arithmetic  31.3 us
    dot_general x26, matrix products, place_field(): jnp.dot(placing.astype(jnp.bfloat16), grads, preferred_element_type=jnp.f...  30.5 us
    dot_general x26, matrix products, place_field(): jnp.dot(placing.astype(jnp.float32), shifted, precision=lax.Precision.HIG...  26.3 us
    dynamic_slice x26, local copies, waits for them, and re-layouts, tally_rows(): return lax.map(per_field, (arrived, row_tags))  19.9 us
  transfers between devices with their start and end apart: 4, of which 2 were waited for; matrix products, arithmetic and copies ran while one was open for 6% of the time, Pallas kernels for 0%

profile of v1, /device:TPU:0, one launch (start us, length us, event | category | flops | bytes accessed | tf_op | source)
XLA Modules:
  0.0 539.1 jit_solution(4381882990473123766)
XLA Ops:
  0.7 2.7 convolution_convert_fusion
  3.4 2.2 reshape.118
  5.6 7.5 %copy.36 = bf16[27,27,512]{1,0,2:T(8,128)(2,1)} copy(bf16[27,27,512]{2,1,0:T(8,128)(2,1)} %reshape.118) | data formatting | bytes 1492992 | tf_op jit(solution)/shard_map/reshape | solution.py:52
  13.1 4.5 fusion.25
  20.9 173.3 %while.25 = (s32[]{:T(128)}, bf16[26,1024,128]{2,1,0:T(8,128)(2,1)}, s32[26,1024]{1,0:T(8,128)}, s32[26,512]{1,0:T(8,128)}, bf16[26,512,128]{2,1,0:T(8,128)(2,1)S(1)}, /*index=5*/s32[]{:T(128)}, s32[]{:T(128)}) while((s32[]{:T(128)}, bf16[26,1024,128]{2,1,0:T(8,128)(2,1)}, s32[26,1024]{1,0:T(8,128)}, s32[26,512]{1,0:T(8,128)}, ...), condition=%wide.region_4.5_spmd, body=%wide.region_0.4_spmd.sunk | while | flops 143897568 | bytes 717545 | solution.py:69
  196.4 7.2 %all-to-all-start = ((s32[8,1,3328]{2,1,0:T(1,128)}), s32[8,1,3328]{2,1,0:T(1,128)S(1)}, u32[]{:S(2)}, u32[]{:S(2)}) async-start(s32[8,1,3328]{2,1,0:T(1,128)} %reshape.128), calls=%async_computation | async-start | bytes 212992 | tf_op jit(solution)/shard_map/all_to_all | solution.py:86
  203.6 2.3 fusion.35
  205.9 2.3 fusion.34
  208.2 2.2 fusion.33
  210.4 2.2 fusion.32
  216.5 6.0 %all-to-all-start.2 = ((bf16[8,26,1,4,32,128]{5,4,3,1,2,0:T(8,128)(2,1)}), bf16[8,26,1,4,32,128]{5,4,3,1,2,0:T(8,128)(2,1)}, u32[]{:S(2)}, u32[]{:S(2)}) async-start(bf16[8,26,1,4,32,128]{5,4,3,1,2,0:T(8,128)(2,1)} %fusion.28), calls=%async_computation.2 | async-start | bytes 13631488 | tf_op jit(solution)/shard_map/all_to_all | solution.py:75
  225.1 146.3 %all-to-all-done.2 = bf16[8,26,1,4,32,128]{5,4,3,1,2,0:T(8,128)(2,1)} async-done(((bf16[8,26,1,4,32,128]{5,4,3,1,2,0:T(8,128)(2,1)}), bf16[8,26,1,4,32,128]{5,4,3,1,2,0:T(8,128)(2,1)}, u32[]{:S(2)}, u32[]{:S(2)}) %all-to-all-start.2) | async-done | bytes 6815776 | tf_op jit(solution)/shard_map/all_to_all | solution.py:75
  371.5 3.5 all-to-all-start.1
  375.0 7.9 %copy.49 = bf16[26,8,4,32,128]{4,3,1,0,2:T(8,128)(2,1)} copy(bf16[26,8,4,32,128]{4,3,2,0,1:T(8,128)(2,1)} %bitcast.25) | data formatting | bytes 13631488 | tf_op jit(solution)/shard_map/reshape | solution.py:74
  382.9 5.4 %all-to-all-start.3 = ((bf16[26,8,4,32,128]{4,3,1,0,2:T(8,128)(2,1)}), bf16[26,8,4,32,128]{4,3,1,0,2:T(8,128)(2,1)}, u32[]{:S(2)}, u32[]{:S(2)}) async-start(bf16[26,8,4,32,128]{4,3,1,0,2:T(8,128)(2,1)} %copy.49), calls=%async_computation.3 | async-start | bytes 13631488 | tf_op jit(solution)/shard_map/all_to_all | solution.py:73
  388.3 2.4 slice.25
  392.7 2.1 reshape.120
  394.9 69.7 %all-to-all-done.3 = bf16[26,8,4,32,128]{4,3,1,0,2:T(8,128)(2,1)} async-done(((bf16[26,8,4,32,128]{4,3,1,0,2:T(8,128)(2,1)}), bf16[26,8,4,32,128]{4,3,1,0,2:T(8,128)(2,1)}, u32[]{:S(2)}, u32[]{:S(2)}) %all-to-all-start.3) | async-done | bytes 6815776 | tf_op jit(solution)/shard_map/all_to_all | solution.py:73
  464.6 7.9 %copy.50 = bf16[26,8,4,32,128]{4,3,2,1,0:T(8,128)(2,1)} copy(bf16[26,8,4,32,128]{4,3,1,0,2:T(8,128)(2,1)} %all-to-all-done.3) | data formatting | bytes 13631488 | tf_op jit(solution)/shard_map/all_to_all | solution.py:73
  472.4 66.7 %while.26 = (s32[]{:T(128)}, f32[26,128,128]{2,1,0:T(8,128)}, s32[26,1024]{1,0:T(8,128)}, bf16[26,1024,128]{2,1,0:T(8,128)(2,1)}, s32[]{:T(128)}) while((s32[]{:T(128)}, f32[26,128,128]{2,1,0:T(8,128)}, s32[26,1024]{1,0:T(8,128)}, bf16[26,1024,128]{2,1,0:T(8,128)(2,1)}, s32[]{:T(128)}) %tuple.59), condition=%wide.region_6.7_spmd, body=%wide.region_5.6_spmd.sunk | while | flops 33685504 | bytes 341065 | solution.py:43
  473.2 1.8 fusion.57
  475.8 1.8 fusion.57
  478.3 1.8 fusion.57
  493.7 1.8 fusion.57
  496.3 1.8 fusion.57
  498.8 1.8 fusion.57
  504.0 1.8 fusion.57
  514.2 1.8 fusion.57
  516.8 1.8 fusion.57
  524.5 1.8 fusion.57
  534.7 1.8 fusion.57
  537.3 1.8 fusion.57
  (460 shorter events, 231.6 us)
Async XLA Ops:
  0.6 12.5 %copy-start = (bf16[512,27,128]{2,0,1:T(8,128)(2,1)S(1)}, bf16[512,27,128]{2,0,1:T(8,128)(2,1)}, u32[]{:S(2)}) copy-start(bf16[512,27,128]{2,0,1:T(8,128)(2,1)} %param.9) | copy-start | bytes 10616836
  17.7 3.2 copy-start.2
  196.4 20.1 %all-to-all-start = ((s32[8,1,3328]{2,1,0:T(1,128)}), s32[8,1,3328]{2,1,0:T(1,128)S(1)}, u32[]{:S(2)}, u32[]{:S(2)}) async-start(s32[8,1,3328]{2,1,0:T(1,128)} %reshape.128), calls=%async_computation | async-start | bytes 212992 | tf_op jit(solution)/shard_map/all_to_all | solution.py:86
  203.6 9.0 %copy-start.3 = (bf16[26,1024,128]{2,1,0:T(8,128)(2,1)S(1)}, bf16[26,1024,128]{2,1,0:T(8,128)(2,1)}, u32[]{:S(2)}) copy-start(bf16[26,1024,128]{2,1,0:T(8,128)(2,1)} %get-tuple-element.117) | copy-start | bytes 20447236
  216.5 155.0 %all-to-all-start.2 = ((bf16[8,26,1,4,32,128]{5,4,3,1,2,0:T(8,128)(2,1)}), bf16[8,26,1,4,32,128]{5,4,3,1,2,0:T(8,128)(2,1)}, u32[]{:S(2)}, u32[]{:S(2)}) async-start(bf16[8,26,1,4,32,128]{5,4,3,1,2,0:T(8,128)(2,1)} %fusion.28), calls=%async_computation.2 | async-start | bytes 13631488 | tf_op jit(solution)/shard_map/all_to_all | solution.py:75
  371.5 11.4 %all-to-all-start.1 = ((s32[4,1,6656]{2,1,0:T(1,128)}), s32[4,1,6656]{2,1,0:T(1,128)S(1)}, u32[]{:S(2)}, u32[]{:S(2)}) async-start(s32[4,1,6656]{2,1,0:T(1,128)} %reshape.130), calls=%async_computation.1 | async-start | bytes 212992 | tf_op jit(solution)/shard_map/all_to_all | solution.py:85
  382.9 81.7 %all-to-all-start.3 = ((bf16[26,8,4,32,128]{4,3,1,0,2:T(8,128)(2,1)}), bf16[26,8,4,32,128]{4,3,1,0,2:T(8,128)(2,1)}, u32[]{:S(2)}, u32[]{:S(2)}) async-start(bf16[26,8,4,32,128]{4,3,1,0,2:T(8,128)(2,1)} %copy.49), calls=%async_computation.3 | async-start | bytes 13631488 | tf_op jit(solution)/shard_map/all_to_all | solution.py:73
  392.7 146.4 %copy-start.1 = (bf16[512,27,128]{2,0,1:T(8,128)(2,1)S(1)}, bf16[512,27,128]{2,0,1:T(8,128)(2,1)}, u32[]{:S(2)}) copy-start(bf16[512,27,128]{2,0,1:T(8,128)(2,1)} %param.9) | copy-start | bytes 10616836
